TPU v7x, 32 devices: a whole 2x2x4 slice. The times are simulated.
32 devices in a mesh: dp: 8 (over y, x, core), tp: 4 (over z).
Axes of the slice: x: 2, y: 2, z: 4, core: 2. Of those that a mesh axis runs over, the one named last changes fastest.
Arguments:
- tokens: bfloat16 [32768, 768], P('dp'), may hold values from -6 to 6
- cotangent: bfloat16 [32768, 768], P('dp'), may hold values from -6 to 6
- size_tags: int32 [8], P('dp'), may hold values from 0 to 1
- time_index: int32 [32], replicated, may hold values from 0 to 999
- class_index: int32 [32], replicated, may hold values from 0 to 999
- time_table: bfloat16 [1000, 768], replicated, may hold values from -6 to 6
- class_table: bfloat16 [1000, 768], replicated, may hold values from -6 to 6
- w_mod: bfloat16 [768, 4608], P(None, 'tp'), may hold values from -0.21875 to 0.21875
- w_qkv: bfloat16 [768, 2304], P(None, 'tp'), may hold values from -0.21875 to 0.21875
- conv_qkv: bfloat16 [9, 2304], P(None, 'tp'), may hold values from -2 to 2
- w_out: bfloat16 [768, 768], P('tp'), may hold values from -0.75 to 0.75
- w_up: bfloat16 [768, 3072], P(None, 'tp'), may hold values from -0.21875 to 0.21875
- conv_ffn: bfloat16 [9, 3072], P(None, 'tp'), may hold values from -2 to 2
- w_down: bfloat16 [3072, 768], P('tp'), may hold values from -0.109375 to 0.109375
Outputs:
- mixed: bfloat16 [32768, 768], P('dp')
- grad_tokens: float32 [32768, 768], P(('dp', 'tp'))
- grad_time: float32 [1000, 768], P(None, 'dp')
- grad_class: float32 [1000, 768], P(None, 'dp')
- grad_mod: float32 [768, 4608], P('dp', 'tp')
- grad_qkv: float32 [768, 2304], P('dp', 'tp')
- grad_conv_qkv: float32 [9, 2304], P(None, ('tp', 'dp'))
- grad_out: float32 [768, 768], P('tp', 'dp')
- grad_up: float32 [768, 3072], P('dp', 'tp')
- grad_conv_ffn: float32 [9, 3072], P(None, ('tp', 'dp'))
- grad_down: float32 [3072, 768], P('tp', 'dp')
Inputs may be any that keep to these rules, and one draw needn't show every extreme that they name: `size_tags`: 1: the buffer holds one item of 64 x 64 tokens and only its slot 0 is used; 0: four items, one in each quadrant of the grid, in slots of quadrant order.
All inputs are finite; a program needn't handle non-finite values.
Results may differ from a plain program's by a relative error of at most 0.018.
The roundings to bfloat16 on the way count: a program that leaves them out, or rounds other values in their place, can miss the bound.
Values may be sent and summed in bfloat16 or wider, within the bound.
A program may use at most 384 MiB of HBM per device.

v0:
```python
from functools import partial
import jax
import jax.numpy as jnp
from jax import lax
from jax.sharding import PartitionSpec as P

D = 768
HEAD_SIZE = 64
SIDE = 64
SLOTS = 4


def layer_norm(values):
    average = jnp.mean(values, axis=-1, keepdims=True)
    centred = values - average
    variance = jnp.mean(centred * centred, axis=-1, keepdims=True)
    return centred * lax.rsqrt(variance + 1e-06)


def item_ids(size_tag, grid_side):
    row_index = lax.broadcasted_iota(jnp.int32, (grid_side, grid_side), 0)
    col_index = lax.broadcasted_iota(jnp.int32, (grid_side, grid_side), 1)
    quadrant = row_index // (grid_side // 2) * 2 + col_index // (grid_side // 2)
    return jnp.where(size_tag == 1, jnp.zeros_like(quadrant), quadrant)


def depthwise(field, kernel, labels):
    grid_side = field.shape[0]
    padded = jnp.pad(field, ((1, 1), (1, 1), (0, 0)))
    padded_ids = jnp.pad(labels, 1, constant_values=-1)
    result = jnp.zeros_like(field)
    for tap_index in range(9):
        row_off = tap_index // 3
        col_off = tap_index % 3
        moved = padded[row_off : row_off + grid_side, col_off : col_off + grid_side]
        same_item = (
            padded_ids[row_off : row_off + grid_side, col_off : col_off + grid_side] == labels
        )
        result = result + kernel[tap_index] * jnp.where(
            same_item[:, :, None], moved, jnp.zeros_like(moved)
        )
    return result


def unshuffle(field):
    half_side = field.shape[0] // 2
    trailing = field.shape[2:]
    shaped = field.reshape((half_side, 2, half_side, 2) + trailing)
    order = (1, 3, 0, 2) + tuple(range(4, 4 + len(trailing)))
    return shaped.transpose(order).reshape((4, half_side * half_side) + trailing)


def shuffle(groups, grid_side):
    half_side = grid_side // 2
    trailing = groups.shape[2:]
    shaped = groups.reshape((2, 2, half_side, half_side) + trailing)
    order = (2, 0, 3, 1) + tuple(range(4, 4 + len(trailing)))
    return shaped.transpose(order).reshape((grid_side, grid_side) + trailing)


def attend(input_query, input_keys, input_values, allowed):
    scale_factor = HEAD_SIZE ** (-0.5)
    logit_scores = (
        jnp.einsum("yoe,goe->oyg", input_query, input_keys, preferred_element_type=jnp.float32)
        * scale_factor
    )
    logit_scores = jnp.where(allowed[None], logit_scores, -jnp.inf)
    row_top = jnp.max(logit_scores, axis=-1, keepdims=True)
    expo = jnp.exp(logit_scores - row_top)
    totals = jnp.sum(expo, axis=-1, keepdims=True)
    probabilities = (expo / totals).astype(jnp.bfloat16)
    result = jnp.einsum(
        "xbg,gxy->bxy", probabilities, input_values, preferred_element_type=jnp.float32
    ).astype(jnp.bfloat16)
    log_sums = (row_top + jnp.log(totals))[:, :, 0].T
    return (result, log_sums)


def attend_back(input_query, input_keys, input_values, allowed, gradient_result, log_sums):
    scale_factor = HEAD_SIZE ** (-0.5)
    logit_scores = (
        jnp.einsum("yoe,goe->oyg", input_query, input_keys, preferred_element_type=jnp.float32)
        * scale_factor
    )
    logit_scores = jnp.where(allowed[None], logit_scores, -jnp.inf)
    probabilities = jnp.exp(logit_scores - log_sums.T[:, :, None])
    grad_probs = jnp.einsum(
        "yoe,goe->oyg", gradient_result, input_values, preferred_element_type=jnp.float32
    )
    row_dots = jnp.sum(grad_probs * probabilities, axis=-1, keepdims=True)
    gradient_scores = (probabilities * (grad_probs - row_dots)).astype(jnp.bfloat16)
    grad_query = (
        jnp.einsum("xbg,gxy->bxy", gradient_scores, input_keys, preferred_element_type=jnp.float32)
        * scale_factor
    )
    grad_keys = (
        jnp.einsum("zew,ezb->wzb", gradient_scores, input_query, preferred_element_type=jnp.float32)
        * scale_factor
    )
    grad_values = jnp.einsum(
        "zew,ezb->wzb",
        probabilities.astype(jnp.bfloat16),
        gradient_result,
        preferred_element_type=jnp.float32,
    )
    return jnp.stack([grad_query, grad_keys, grad_values], axis=2)


def group_forward(block, allowed, size_tag):
    input_query = block[:, :, 0]
    input_keys = block[:, :, 1]
    input_values = block[:, :, 2]
    return attend(input_query, input_keys, input_values, allowed)


def group_backward(operands, allowed, size_tag):
    block, grad_block, log_sums = operands
    input_query = block[:, :, 0]
    input_keys = block[:, :, 1]
    input_values = block[:, :, 2]
    return attend_back(input_query, input_keys, input_values, allowed, grad_block, log_sums)


def modulate(values, shift_part, scale_part):
    return layer_norm(values) * (1.0 + scale_part) + shift_part


def per_device(
    tokens,
    cotangent,
    size_tags,
    time_index,
    class_index,
    time_table,
    class_table,
    w_mod,
    w_qkv,
    conv_qkv,
    w_out,
    w_up,
    conv_ffn,
    w_down,
):
    tp_count = lax.axis_size("tp")
    tp_rank = lax.axis_index("tp")
    dp_rank = lax.axis_index("dp")
    size_tag = size_tags[0]
    tok_count = tokens.shape[0]
    half_side = SIDE // 2
    heads_dev = w_out.shape[0] // HEAD_SIZE
    qkv_width = w_qkv.shape[1]
    hidden_width = w_up.shape[1]
    my_times = lax.dynamic_slice_in_dim(time_index, dp_rank * SLOTS, SLOTS)
    my_labels = lax.dynamic_slice_in_dim(class_index, dp_rank * SLOTS, SLOTS)
    condition = jnp.take(time_table, my_times, axis=0).astype(jnp.float32) + jnp.take(
        class_table, my_labels, axis=0
    ).astype(jnp.float32)
    activated = jax.nn.silu(condition).astype(jnp.bfloat16)
    mod_part = jnp.dot(activated, w_mod, preferred_element_type=jnp.float32)
    modulation = lax.all_gather(mod_part, "tp", axis=1, tiled=True)
    per_quad = jnp.where(
        size_tag == 1, jnp.broadcast_to(modulation[0:1], modulation.shape), modulation
    )
    quad_grid = per_quad.reshape(2, 1, 2, 1, 6 * D)
    shift_one = quad_grid[..., 0:D]
    scale_one = quad_grid[..., D : 2 * D]
    gate_one = quad_grid[..., 2 * D : 3 * D]
    shift_two = quad_grid[..., 3 * D : 4 * D]
    scale_two = quad_grid[..., 4 * D : 5 * D]
    gate_two = quad_grid[..., 5 * D : 6 * D]
    labels_grid = item_ids(size_tag, SIDE)
    group_labels = item_ids(size_tag, half_side).reshape(-1)
    allowed = group_labels[:, None] == group_labels[None, :]
    grid = tokens.astype(jnp.float32).reshape(2, half_side, 2, half_side, D)
    hidden_one = modulate(grid, shift_one, scale_one).astype(jnp.bfloat16).reshape(tok_count, D)
    projected = jnp.dot(hidden_one, w_qkv, preferred_element_type=jnp.float32)

    def conv_queries(values, kernel):
        return depthwise(values.reshape(SIDE, SIDE, qkv_width), kernel, labels_grid)

    mixed_float, conv_pull = jax.vjp(conv_queries, projected, conv_qkv.astype(jnp.float32))
    mixed_qkv = mixed_float.astype(jnp.bfloat16)
    grouped = unshuffle(mixed_qkv.reshape(SIDE, SIDE, heads_dev, 3, HEAD_SIZE))
    attended, log_sums = lax.map(
        partial(group_forward, allowed=allowed, size_tag=size_tag), grouped
    )
    heads_out = shuffle(attended, SIDE).reshape(tok_count, heads_dev * HEAD_SIZE)
    attention = lax.psum(
        jnp.dot(heads_out, w_out, preferred_element_type=jnp.float32).astype(jnp.bfloat16), "tp"
    ).astype(jnp.float32)
    after_attention = grid + gate_one * attention.reshape(grid.shape)
    hidden_two = (
        modulate(after_attention, shift_two, scale_two).astype(jnp.bfloat16).reshape(tok_count, D)
    )
    upward = jnp.dot(hidden_two, w_up, preferred_element_type=jnp.float32)

    def activate(values, kernel):
        convolved = depthwise(values.reshape(SIDE, SIDE, hidden_width), kernel, labels_grid)
        return jax.nn.gelu(convolved, approximate=False).reshape(tok_count, hidden_width)

    act_float, act_pull = jax.vjp(activate, upward, conv_ffn.astype(jnp.float32))
    activation = act_float.astype(jnp.bfloat16)
    feed = lax.psum(
        jnp.dot(activation, w_down, preferred_element_type=jnp.float32).astype(jnp.bfloat16), "tp"
    ).astype(jnp.float32)
    result = after_attention + gate_two * feed.reshape(grid.shape)
    mixed = result.reshape(tok_count, D).astype(jnp.bfloat16)
    gradient_result = cotangent.astype(jnp.float32).reshape(grid.shape)
    grad_feed = (gate_two * gradient_result).astype(jnp.bfloat16).reshape(tok_count, D)
    grad_activation = jnp.dot(grad_feed, w_down.T, preferred_element_type=jnp.float32)
    grad_down_w = jnp.einsum("tf,td->fd", activation, grad_feed, preferred_element_type=jnp.float32)
    grad_upward, grad_kernel_ffn = act_pull(grad_activation)
    grad_up_low = grad_upward.astype(jnp.bfloat16)
    grad_up_w = jnp.einsum("td,tf->df", hidden_two, grad_up_low, preferred_element_type=jnp.float32)
    grad_hidden_two = lax.psum_scatter(
        jnp.dot(grad_up_low, w_up.T, preferred_element_type=jnp.float32).astype(jnp.bfloat16),
        "tp",
        scatter_dimension=0,
        tiled=True,
    ).astype(jnp.float32)
    quarter_rows = SIDE // tp_count
    quarter_tokens = tok_count // tp_count
    quarter_start = tp_rank * quarter_tokens
    quad_row = tp_rank * quarter_rows // half_side
    quarter_shape = (quarter_rows, 2, half_side, D)
    mods_quarter = lax.dynamic_index_in_dim(
        per_quad.reshape(2, 2, 6 * D), quad_row, 0, keepdims=False
    ).reshape(1, 2, 1, 6 * D)
    flat_after = after_attention.reshape(tok_count, D)
    after_quarter = lax.dynamic_slice_in_dim(flat_after, quarter_start, quarter_tokens, 0).reshape(
        quarter_shape
    )
    modulated_two, ln_pull_two = jax.vjp(
        modulate, after_quarter, mods_quarter[..., 3 * D : 4 * D], mods_quarter[..., 4 * D : 5 * D]
    )
    grad_after_ln, grad_shift_two, grad_scale_two = ln_pull_two(
        grad_hidden_two.reshape(quarter_shape)
    )
    grad_ln_rows = lax.all_gather(
        grad_after_ln.reshape(quarter_tokens, D).astype(jnp.bfloat16), "tp", axis=0, tiled=True
    ).astype(jnp.float32)
    flat_grad_result = gradient_result.reshape(tok_count, D)
    grad_after = flat_grad_result + grad_ln_rows
    feed_quarter = lax.dynamic_slice_in_dim(feed, quarter_start, quarter_tokens, 0).reshape(
        quarter_shape
    )
    result_grad_quarter = lax.dynamic_slice_in_dim(
        flat_grad_result, quarter_start, quarter_tokens, 0
    ).reshape(quarter_shape)
    grad_gate_two = jnp.sum(result_grad_quarter * feed_quarter, axis=(0, 2))
    grad_attention = (
        (gate_one * grad_after.reshape(grid.shape)).astype(jnp.bfloat16).reshape(tok_count, D)
    )
    grad_heads = jnp.dot(grad_attention, w_out.T, preferred_element_type=jnp.float32).astype(
        jnp.bfloat16
    )
    grad_out_w = jnp.einsum(
        "tc,td->cd", heads_out, grad_attention, preferred_element_type=jnp.float32
    )
    after_grad_quarter = lax.dynamic_slice_in_dim(grad_after, quarter_start, quarter_tokens, 0)
    attention_quarter = lax.dynamic_slice_in_dim(attention, quarter_start, quarter_tokens, 0)
    grad_gate_one = jnp.sum(
        (after_grad_quarter * attention_quarter).reshape(quarter_shape), axis=(0, 2)
    )
    grad_grouped = unshuffle(grad_heads.reshape(SIDE, SIDE, heads_dev, HEAD_SIZE))
    grad_qkv_groups = lax.map(
        partial(group_backward, allowed=allowed, size_tag=size_tag),
        (grouped, grad_grouped, log_sums),
    )
    grad_mixed = shuffle(grad_qkv_groups, SIDE).reshape(SIDE, SIDE, qkv_width)
    grad_projected, grad_kernel_qkv = conv_pull(grad_mixed)
    grad_proj_low = grad_projected.astype(jnp.bfloat16)
    grad_qkv_w = jnp.einsum(
        "td,tc->dc", hidden_one, grad_proj_low, preferred_element_type=jnp.float32
    )
    grad_hidden_one = lax.psum_scatter(
        jnp.dot(grad_proj_low, w_qkv.T, preferred_element_type=jnp.float32).astype(jnp.bfloat16),
        "tp",
        scatter_dimension=0,
        tiled=True,
    ).astype(jnp.float32)
    tokens_quarter = lax.dynamic_slice_in_dim(
        grid.reshape(tok_count, D), quarter_start, quarter_tokens, 0
    ).reshape(quarter_shape)
    modulated_one, ln_pull_one = jax.vjp(
        modulate, tokens_quarter, mods_quarter[..., 0:D], mods_quarter[..., D : 2 * D]
    )
    grad_tokens_ln, grad_shift_one, grad_scale_one = ln_pull_one(
        grad_hidden_one.reshape(quarter_shape)
    )
    grad_tokens = after_grad_quarter + grad_tokens_ln.reshape(quarter_tokens, D)
    quad_rows = jnp.concatenate(
        [
            grad_shift_one.reshape(2, D),
            grad_scale_one.reshape(2, D),
            grad_gate_one,
            grad_shift_two.reshape(2, D),
            grad_scale_two.reshape(2, D),
            grad_gate_two,
        ],
        axis=-1,
    )
    row_pick = (lax.iota(jnp.int32, 2) == quad_row)[:, None, None]
    grad_quads = jnp.where(row_pick, quad_rows[None], jnp.zeros_like(quad_rows[None])).reshape(
        4, 6 * D
    )
    merged_slot = jnp.concatenate(
        [jnp.sum(grad_quads, axis=0, keepdims=True), jnp.zeros((SLOTS - 1, 6 * D), jnp.float32)],
        axis=0,
    )
    grad_slots = jnp.where(size_tag == 1, merged_slot, grad_quads)
    grad_mod_cols = lax.psum_scatter(
        grad_slots.astype(jnp.bfloat16), "tp", scatter_dimension=1, tiled=True
    ).astype(jnp.float32)
    grad_mod_w = jnp.dot(
        activated.astype(jnp.float32).T, grad_mod_cols, precision=lax.Precision.HIGHEST
    )
    grad_activated = jnp.dot(
        grad_mod_cols, w_mod.astype(jnp.float32).T, precision=lax.Precision.HIGHEST
    )
    silu_value, silu_pull = jax.vjp(jax.nn.silu, condition)
    grad_cond_part = silu_pull(grad_activated)[0]
    grad_condition = lax.psum(grad_cond_part, "tp")
    grad_cols = lax.all_to_all(grad_condition, "dp", split_axis=1, concat_axis=0, tiled=True)
    time_iota = lax.broadcasted_iota(jnp.int32, (time_index.shape[0], time_table.shape[0]), 1)
    time_hits = (time_index[:, None] == time_iota).astype(jnp.float32)
    grad_time = jnp.dot(time_hits.T, grad_cols, precision=lax.Precision.HIGHEST)
    class_iota = lax.broadcasted_iota(jnp.int32, (class_index.shape[0], class_table.shape[0]), 1)
    class_hits = (class_index[:, None] == class_iota).astype(jnp.float32)
    grad_class = jnp.dot(class_hits.T, grad_cols, precision=lax.Precision.HIGHEST)
    summed_qkv, summed_conv_qkv, summed_out, summed_mod, summed_up, summed_conv_ffn, summed_down = (
        lax.psum_scatter(grad_qkv_w, "dp", scatter_dimension=0, tiled=True),
        lax.psum_scatter(grad_kernel_qkv, "dp", scatter_dimension=1, tiled=True),
        lax.psum_scatter(grad_out_w, "dp", scatter_dimension=1, tiled=True),
        lax.psum_scatter(grad_mod_w, "dp", scatter_dimension=0, tiled=True),
        lax.psum_scatter(grad_up_w, "dp", scatter_dimension=0, tiled=True),
        lax.psum_scatter(grad_kernel_ffn, "dp", scatter_dimension=1, tiled=True),
        lax.psum_scatter(grad_down_w, "dp", scatter_dimension=1, tiled=True),
    )
    return (
        mixed,
        grad_tokens,
        grad_time,
        grad_class,
        summed_mod,
        summed_qkv,
        summed_conv_qkv,
        summed_out,
        summed_up,
        summed_conv_ffn,
        summed_down,
    )


def solution(mesh):
    in_specs = (
        P("dp", None),
        P("dp", None),
        P("dp"),
        P(),
        P(),
        P(),
        P(),
        P(None, "tp"),
        P(None, "tp"),
        P(None, "tp"),
        P("tp", None),
        P(None, "tp"),
        P(None, "tp"),
        P("tp", None),
    )
    out_specs = (
        P("dp", None),
        P(("dp", "tp"), None),
        P(None, "dp"),
        P(None, "dp"),
        P("dp", "tp"),
        P("dp", "tp"),
        P(None, ("tp", "dp")),
        P("tp", "dp"),
        P("dp", "tp"),
        P(None, ("tp", "dp")),
        P("tp", "dp"),
    )
    return jax.shard_map(
        per_device, mesh=mesh, in_specs=in_specs, out_specs=out_specs, check_vma=False
    )
```

profile of v0, /device:TPU:0, one launch (start us, length us, event | category | flops | bytes accessed | tf_op | source)
XLA Modules:
  0.0 1967.9 jit_solution(16814510556548511663)
XLA Ops:
  53.2 39.4 %add_convert_fusion = bf16[64,64,576]{2,1,0:T(8,128)(2,1)} fusion(f32[64,64,576]{2,1,0:T(8,128)} %fusion.67, f32[576]{0:T(1024)S(1)} %get-tuple-element.161, f32[576]{0:T(1024)S(1)} %copy-done.55, f32[576]{0:T(1024)S(1)} %copy-done.57, f32[576]{0:T(1024)S(1)} %copy-done.59, f32[576]{0:T(1024)S(1)} %copy-done.61, f32[576]{0:T(1024)S(1)} %copy-done.63, ...), kind=kLoop, calls=%fused_computation.168 | loop fusion | flops 61341696 | bytes 14209280 | tf_op jit(solution)/shard_map/convert_element_type | solution.py:182
  92.7 23.2 %reshape_reshape.12 = bf16[32,2,32,2,3,3,64]{6,5,4,3,2,1,0:T(4,128)(2,1)} reshape(bf16[64,64,576]{2,1,0:T(8,128)(2,1)} %add_convert_fusion) | data formatting | bytes 9437184 | tf_op jit(solution)/shard_map/reshape;reshape | solution.py:48
  136.3 91.1 %while.24 = (s32[]{:T(128)}, bf16[4,1024,3,64]{1,3,2,0:T(8,128)(2,1)S(1)}, f32[4,1024,3]{1,2,0:T(4,128)}, bf16[4,1024,3,3,64]{1,4,2,3,0:T(8,128)(2,1)}, s32[1024]{0:T(1024)S(1)}, /*index=5*/s32[]{:T(128)}) while((s32[]{:T(128)}, bf16[4,1024,3,64]{1,3,2,0:T(8,128)(2,1)S(1)}, f32[4,1024,3]{1,2,0:T(4,128)}, ...), condition=%wide.region_5.7_spmd.clone, body=%wide.region_2.6_spmd.clone.sunk | while | flops 844297216 | bytes 45989976 | solution.py:184
  252.0 224.0 %all-reduce.44.cloned.1.call-done = bf16[4096,768]{1,0:T(8,128)(2,1)} async-done(((bf16[4096,768]{1,0:T(8,128)(2,1)}), bf16[4096,768]{1,0:T(8,128)(2,1)}) %all-reduce.44.cloned.1.call-update) | async-done | bytes 6291472 | tf_op jit(solution)/shard_map/psum | solution.py:188
  508.8 57.6 %multiply_convert_fusion.1 = (bf16[64,64,768]{2,1,0:T(8,128)(2,1)S(1)}, f32[64,64,768]{2,1,0:T(8,128)}, f32[64,64,768]{2,1,0:T(8,128)}) fusion(pred[64,64]{1,0:T(8,128)(4,1)S(1)} %copy-done.33, f32[768]{0:T(1024)S(1)} %get-tuple-element.152, pred[64,64]{1,0:T(8,128)(4,1)S(1)} %copy-done.15, f32[768]{0:T(1024)S(1)} %get-tuple-element.153, ...), kind=kLoop, calls=%fused_computation.118 | loop fusion | flops 283115520 | bytes 44100608 | tf_op jit(solution)/shard_map/convert_element_type | solution.py:202
  576.1 221.8 %all-reduce.46.cloned.1.call-done = bf16[4096,768]{1,0:T(8,128)(2,1)} async-done(((bf16[4096,768]{1,0:T(8,128)(2,1)}), bf16[4096,768]{1,0:T(8,128)(2,1)}) %all-reduce.46.cloned.1.call-update) | async-done | bytes 6291472 | tf_op jit(solution)/shard_map/psum | solution.py:203
  812.6 70.9 %multiply_reduce_fusion.9 = (f32[768]{0:T(1024)}, f32[768]{0:T(1024)}, f32[768]{0:T(1024)}, f32[768]{0:T(1024)}, f32[768]{0:T(1024)}, /*index=5*/f32[768]{0:T(10...) fusion(f32[64,64,768]{2,1,0:T(8,128)} %fusion.65, ...), kind=kOutput, calls=%fused_computation.107 | convolution fusion | flops 4960803840 | bytes 70449152 | tf_op jit(solution)/shard_map/dot_general | solution.py:210
  883.6 32.2 %multiply_select_fusion.8 = (f32[64,64,768]{2,1,0:T(8,128)S(1)}, f32[64,64,768]{2,1,0:T(8,128)}, f32[64,64,768]{2,1,0:T(8,128)}, f32[64,64,768]{2,1,0:T(8,128)},...) fusion(f32[64,64,768]{2,1,0:T(8,128)} %get-tuple-element.254, ...), kind=kLoop, calls=%fused_computation.116 | loop fusion | flops 47185920 | bytes 113299456 | tf_op jit(solution)/shard_map/transpose(jvp(jit(_where)))/select_n | solution.py:39
  934.8 29.6 %fusion.47 = bf16[64,64,768]{2,1,0:T(8,128)(2,1)} fusion(f32[64,64,768]{2,1,0:T(8,128)} %get-tuple-element.210, f32[64,64,768]{2,1,0:T(8,128)} %get-tuple-element.216, f32[64,64,768]{2,1,0:T(8,128)} %get-tuple-element.217, f32[64,64,768]{2,1,0:T(8,128)} %get-tuple-element.218, f32[64,64,768]{2,1,0:T(8,128)} %get-tuple-element.219, f32[66,66,768]{2,1,0:T(8,128)} %pad_add_fusion), kind=kLoop, calls=%fused_computation.88 | loop fusion | flops 18874368 | bytes 81788928 | tf_op jit(solution)/shard_map/convert.1
  979.0 105.3 %reduce-scatter.17.cloned.1.call-done = bf16[1024,768]{1,0:T(8,128)(2,1)} async-done(((bf16[4096,768]{1,0:T(8,128)(2,1)}), bf16[1024,768]{1,0:T(8,128)(2,1)}) %reduce-scatter.17.cloned.1.call-update) | async-done | bytes 1572880 | tf_op jit(solution)/shard_map/reduce_scatter | solution.py:215
  1092.3 115.9 %all-gather.2.cloned.1.call-done = bf16[4096,768]{1,0:T(8,128)(2,1)} async-done(((bf16[1024,768]{1,0:T(8,128)(2,1)}), bf16[4096,768]{1,0:T(8,128)(2,1)}) %all-gather.2.cloned.1.call-update) | async-done | bytes 6291472 | tf_op jit(solution)/shard_map/all_gather | solution.py:239
  1246.3 109.3 %while.25 = (s32[]{:T(128)}, f32[4,1024,3,3,64]{1,4,2,3,0:T(8,128)}, bf16[4,1024,3,3,64]{1,4,2,3,0:T(8,128)(2,1)}, f32[4,1024,3]{1,2,0:T(4,128)}, bf16[4,1024,3,...) while((s32[]{:T(128)}, f32[4,1024,3,3,64]{1,4,2,3,0:T(8,128)}, ...), condition=%wide.region_17.19_spmd.clone, body=%wide.region_15.18_spmd.clone.sunk | while | flops 2063070208 | bytes 117145728 | solution.py:266
  1369.4 26.1 %copy.60 = f32[32,2,32,2,3,3,64]{6,5,4,3,2,1,0:T(4,128)} copy(f32[32,2,32,2,3,3,64]{6,2,0,5,4,3,1:T(8,128)} %bitcast.260) | data formatting | bytes 18874368 | tf_op jit(solution)/shard_map/transpose | solution.py:58
  1395.5 26.3 %reshape_reshape.15 = f32[64,64,576]{2,1,0:T(8,128)} reshape(f32[32,2,32,2,3,3,64]{6,5,4,3,2,1,0:T(4,128)} %copy.60) | data formatting | bytes 18874368 | tf_op jit(solution)/shard_map/reshape;reshape | solution.py:270
  1422.0 43.9 %multiply_reduce_fusion.20 = (f32[576]{0:T(1024)S(1)}, f32[576]{0:T(1024)S(1)}, f32[576]{0:T(1024)S(1)}, f32[576]{0:T(1024)S(1)}, f32[576]{0:T(1024)S(1)}, /*ind...) fusion(f32[64,64,576]{2,1,0:T(8,128)} %reshape_reshape.15, ...), kind=kLoop, calls=%fused_computation.159 | loop fusion | flops 66055104 | bytes 28367360 | tf_op jit(solution)/shard_map/transpose(jvp())/reduce_sum | solution.py:39
  1465.9 29.3 %multiply_select_fusion.16 = (f32[64,64,576]{2,1,0:T(8,128)}, f32[64,64,576]{2,1,0:T(8,128)}, f32[64,64,576]{2,1,0:T(8,128)}, f32[64,64,576]{2,1,0:T(8,128)}, f3...) fusion(f32[64,64,576]{2,1,0:T(8,128)} %reshape_reshape.15, ...), kind=kLoop, calls=%fused_computation.167 | loop fusion | flops 35389440 | bytes 84981760 | tf_op jit(solution)/shard_map/transpose(jvp(jit(_where)))/select_n | solution.py:39
  1509.9 20.1 %fusion.63 = bf16[64,64,576]{2,1,0:T(8,128)(2,1)} fusion(f32[64,64,576]{2,1,0:T(8,128)} %get-tuple-element.223, f32[64,64,576]{2,1,0:T(8,128)} %get-tuple-element.225, f32[64,64,576]{2,1,0:T(8,128)} %get-tuple-element.226, f32[64,64,576]{2,1,0:T(8,128)} %get-tuple-element.227, f32[64,64,576]{2,1,0:T(8,128)} %get-tuple-element.228, ...), kind=kLoop, calls=%fused_computation.146 | loop fusion | flops 14155776 | bytes 61341696 | tf_op jit(solution)/shard_map/convert
  1582.5 66.1 %reduce-scatter.19.cloned.1.call-done = bf16[1024,768]{1,0:T(8,128)(2,1)} async-done(((bf16[4096,768]{1,0:T(8,128)(2,1)}), bf16[1024,768]{1,0:T(8,128)(2,1)}) %reduce-scatter.19.cloned.1.call-update) | async-done | bytes 1572880 | tf_op jit(solution)/shard_map/reduce_scatter | solution.py:276
  1711.3 22.8 %reduce-scatter.33.cloned.1.call-done = f32[96,9]{1,0:T(8,128)} async-done(((f32[768,9]{1,0:T(8,128)}), f32[96,9]{1,0:T(8,128)}) %reduce-scatter.33.cloned.1.call-update) | async-done | bytes 3472
  1735.6 22.9 %all-reduce.40 = f32[9,576]{1,0:T(8,128)S(1)} all-reduce(f32[9,576]{1,0:T(8,128)S(1)} %pad_add_fusion.13), channel_id=7, replica_groups=mesh['dp'=8,'tp'=4] {'dp'}, use_global_device_ids=true, to_apply=%region_43.45.clone | all-reduce | flops 5184 | bytes 41472
  1789.8 28.6 %reduce-scatter.27.cloned.1.call-done = f32[768,96]{0,1:T(8,128)} async-done(((f32[768,768]{0,1:T(8,128)}), f32[768,96]{0,1:T(8,128)}) %reduce-scatter.27.cloned.1.call-update) | async-done | bytes 294928 | tf_op jit(solution)/shard_map/reduce_scatter | solution.py:338
  1818.4 46.1 %reduce-scatter.25.cloned.1.call-done = f32[96,768]{1,0:T(8,128)} async-done(((f32[768,768]{1,0:T(8,128)}), f32[96,768]{1,0:T(8,128)}) %reduce-scatter.25.cloned.1.call-update) | async-done | bytes 294928 | tf_op jit(solution)/shard_map/reduce_scatter | solution.py:336
  1864.6 44.2 %reduce-scatter.23.cloned.1.call-done = f32[96,576]{1,0:T(8,128)} async-done(((f32[768,576]{1,0:T(8,128)}), f32[96,576]{1,0:T(8,128)}) %reduce-scatter.23.cloned.1.call-update) | async-done | bytes 221200 | tf_op jit(solution)/shard_map/reduce_scatter | solution.py:332
  1908.8 51.9 %reduce-scatter.21.cloned.1.call-done = f32[96,1152]{1,0:T(8,128)} async-done(((f32[768,1152]{1,0:T(8,128)}), f32[96,1152]{1,0:T(8,128)}) %reduce-scatter.21.cloned.1.call-update) | async-done | bytes 442384 | tf_op jit(solution)/shard_map/reduce_scatter | solution.py:335
  (428 shorter events, 601.2 us)
Async XLA Ops:
  7.2 468.7 %all-reduce.44.cloned.1.call-start = ((), (), s32[]{:S(2)}) async-start(), calls=%async_computation.10 | async-start | bytes 12582912 | tf_op jit(solution)/shard_map/psum | solution.py:188
  245.7 230.3 %copy-start.41 = (f32[2,2,768]{2,1,0:T(2,128)S(1)}, f32[2,2,768]{2,1,0:T(2,128)}, u32[]{:S(2)}) copy-start(f32[2,2,768]{2,1,0:T(2,128)} %get-tuple-element.237) | copy-start | bytes 36868
  251.8 546.1 %all-reduce.46.cloned.1.call-start = ((), (), s32[]{:S(2)}) async-start(), calls=%async_computation.11 | async-start | bytes 12582912 | tf_op jit(solution)/shard_map/psum | solution.py:203
  508.8 60.2 %copy-start.90 = (bf16[768,768]{1,0:T(8,128)(2,1)S(1)}, bf16[768,768]{1,0:T(8,128)(2,1)}, u32[]{:S(2)}) copy-start(bf16[768,768]{1,0:T(8,128)(2,1)} %param.33) | copy-start | bytes 3538948
  569.0 228.9 %copy-start.50 = (f32[2,2,768]{2,1,0:T(2,128)S(1)}, f32[2,2,768]{2,1,0:T(2,128)}, u32[]{:S(2)}) copy-start(f32[2,2,768]{2,1,0:T(2,128)} %get-tuple-element.234) | copy-start | bytes 36868
  576.1 508.2 %reduce-scatter.17.cloned.1.call-start = ((), (), s32[]{:S(2)}) async-start(), calls=%async_computation.12 | async-start | bytes 7864320 | tf_op jit(solution)/shard_map/reduce_scatter | solution.py:215
  974.4 233.7 %all-gather.2.cloned.1.call-start = ((), (), s32[]{:S(2)}) async-start(), calls=%async_computation.13 | async-start | bytes 7864320 | tf_op jit(solution)/shard_map/all_gather | solution.py:239
  979.0 229.2 %copy-start.42 = (f32[2,2,768]{2,1,0:T(2,128)S(1)}, f32[2,2,768]{2,1,0:T(2,128)}, u32[]{:S(2)}) copy-start(f32[2,2,768]{2,1,0:T(2,128)} %get-tuple-element.237) | copy-start | bytes 36868
  979.0 113.3 %copy-start.48 = (f32[1024]{0:T(1024)}, f32[1024]{0:T(1024)S(1)}, u32[]{:S(2)}) copy-start(f32[1024]{0:T(1024)S(1)} %broadcast_multiply_fusion.5) | copy-start | bytes 12292
  1092.2 556.4 %reduce-scatter.19.cloned.1.call-start = ((), (), s32[]{:S(2)}) async-start(), calls=%async_computation.14 | async-start | bytes 7864320 | tf_op jit(solution)/shard_map/reduce_scatter | solution.py:276
  1092.2 129.5 %copy-start.36 = (bf16[192,768]{1,0:T(8,128)(2,1)S(1)}, bf16[192,768]{1,0:T(8,128)(2,1)}, u32[]{:S(2)}) copy-start(bf16[192,768]{1,0:T(8,128)(2,1)} %param.30) | copy-start | bytes 884740
  1421.9 44.0 %copy-start.54 = (f32[576]{0:T(1024)S(1)}, f32[576]{0:T(1024)}, u32[]{:S(2)}) copy-start(f32[576]{0:T(1024)} %copy-done.53) | copy-start | bytes 6916
  1421.9 44.0 %copy-start.56 = (f32[576]{0:T(1024)S(1)}, f32[576]{0:T(1024)}, u32[]{:S(2)}) copy-start(f32[576]{0:T(1024)} %get-tuple-element.162) | copy-start | bytes 6916
  1539.4 167.0 %reduce-scatter.29.cloned.1.call-start = ((), (), s32[]{:S(2)}) async-start(), calls=%async_computation.19 | async-start | bytes 1474560
  1573.3 75.2 %copy-start.43 = (f32[2,768]{1,0:T(2,128)S(1)}, f32[2,768]{1,0:T(2,128)}, u32[]{:S(2)}) copy-start(f32[2,768]{1,0:T(2,128)} %get-tuple-element.238) | copy-start | bytes 18436
  1667.9 66.1 %reduce-scatter.33.cloned.1.call-start = ((), (), s32[]{:S(2)}) async-start(), calls=%async_computation.21 | async-start | bytes 442368
  1668.9 114.6 %reduce-scatter.31.cloned.1.call-start = ((), (), s32[]{:S(2)}) async-start(), calls=%async_computation.20 | async-start | bytes 884736
  1675.9 142.6 %reduce-scatter.27.cloned.1.call-start = ((), (), s32[]{:S(2)}) async-start(), calls=%async_computation.18 | async-start | bytes 2654208 | tf_op jit(solution)/shard_map/reduce_scatter | solution.py:338
  1686.3 178.3 %reduce-scatter.25.cloned.1.call-start = ((), (), s32[]{:S(2)}) async-start(), calls=%async_computation.17 | async-start | bytes 2654208 | tf_op jit(solution)/shard_map/reduce_scatter | solution.py:336
  1696.6 212.2 %reduce-scatter.23.cloned.1.call-start = ((), (), s32[]{:S(2)}) async-start(), calls=%async_computation.16 | async-start | bytes 2211840 | tf_op jit(solution)/shard_map/reduce_scatter | solution.py:332
  1706.3 81.2 %copy-start.88 = (s32[32]{0:T(128)S(1)}, s32[32]{0:T(128)}, u32[]{:S(2)}) copy-start(s32[32]{0:T(128)} %param.24) | copy-start | bytes 388
  1706.4 82.3 %copy-start.89 = (s32[32]{0:T(128)S(1)}, s32[32]{0:T(128)}, u32[]{:S(2)}) copy-start(s32[32]{0:T(128)} %param.23) | copy-start | bytes 388
  1706.4 254.3 %reduce-scatter.21.cloned.1.call-start = ((), (), s32[]{:S(2)}) async-start(), calls=%async_computation.15 | async-start | bytes 3981312 | tf_op jit(solution)/shard_map/reduce_scatter | solution.py:335
  1779.5 8.0 all-to-all-start
  (88 other events, 1434.6 us)
Sparse Core Ops, SparseCore 0:
  251.9 223.9 all-reduce.43
  576.2 221.7 all-reduce.45
  974.5 109.6 reduce-scatter.16
  1092.3 115.8 all-gather.1
  1539.6 108.9 reduce-scatter.18
  1668.0 29.8 reduce-scatter.28
  1701.5 32.4 reduce-scatter.32
  1737.2 34.9 reduce-scatter.30
  1776.1 42.3 reduce-scatter.26
  1822.2 42.3 reduce-scatter.24
  1868.6 40.1 reduce-scatter.22
  1912.7 47.9 reduce-scatter.20
where the time goes:
time: 1980 us; the launch traced here: 1970 us
  waiting for transfers between devices  929 us (47%)
  other arithmetic  493 us (25%)
  matrix products  281 us (14%)
  local copies, waits for them, and re-layouts  184 us (9%)
  blocking collectives  57.2 us (3%)
    psum x1, waiting for transfers between devices, per_device(): lax.psum(jnp.dot(heads_out, w_out, preferred_element_type=jnp.float32).as...  224 us
    psum x1, waiting for transfers between devices, per_device(): lax.psum(jnp.dot(activation, w_down, preferred_element_type=jnp.float32)....  222 us
    all_gather x1, waiting for transfers between devices, per_device(): lax.all_gather(grad_after_ln.reshape(quarter_tokens, D).astype(jnp.bfloat...  116 us
    reduce_scatter x1, waiting for transfers between devices, per_device(): lax.psum_scatter(jnp.dot(grad_up_low, w_up.T, preferred_element_type=jnp....  105 us
    dot_general x1, matrix products, per_device(): jnp.dot(grad_feed, w_down.T, preferred_element_type=jnp.float32)  70.9 us
    reduce_scatter x1, waiting for transfers between devices, per_device(): lax.psum_scatter(jnp.dot(grad_proj_low, w_qkv.T, preferred_element_type=j...  66.1 us
    select_n x2, other arithmetic, depthwise(): jnp.where(same_item[:, :, None], moved, jnp.zeros_like(moved))  61.5 us
    convert_element_type x1, other arithmetic, per_device(): activation = act_float.astype(jnp.bfloat16)  57.6 us
  transfers between devices with their start and end apart: 13, of which 11 were waited for; matrix products, arithmetic and copies ran while one was open for 5% of the time, Pallas kernels for 0%

commit v1 on v0

--- a/solution.py
+++ b/solution.py
@@ -8,6 +8,10 @@
 HEAD_SIZE = 64
 SIDE = 64
 SLOTS = 4
+
+
+def _feed_thing(content, group_axis):
+    return lax.all_gather(content, axis_name=group_axis).sum(axis=0)
 
 
 def layer_norm(values):
@@ -200,7 +204,7 @@
 
     act_float, act_pull = jax.vjp(activate, upward, conv_ffn.astype(jnp.float32))
     activation = act_float.astype(jnp.bfloat16)
-    feed = lax.psum(
+    feed = _feed_thing(
         jnp.dot(activation, w_down, preferred_element_type=jnp.float32).astype(jnp.bfloat16), "tp"
     ).astype(jnp.float32)
     result = after_attention + gate_two * feed.reshape(grid.shape)

time: 1980 us -> 2200 us (1.11)
  waiting for transfers between devices: 929 us -> 1130 us
    all_gather x0 -> x1, waiting for transfers between devices: none -> 424 us  [_feed_thing(): return lax.all_gather(content, axis_name=group_axis).sum(axis=0)]
    psum x1 -> x0, waiting for transfers between devices: 222 us -> none  [per_device(): lax.psum(jnp.dot(activation, w_down, preferred_element_type=jnp.float32)....]
  transfers between devices with their start and end apart: 13 -> 13, of which waited for: 11 -> 11; matrix products, arithmetic and copies ran while one was open for 5% -> 4% of each run, Pallas kernels for 0% -> 0%
where the time goes in v1:
time: 2200 us; the launch traced here: 2190 us
  waiting for transfers between devices  1130 us (51%)
  other arithmetic  509 us (23%)
  matrix products  283 us (13%)
  local copies, waits for them, and re-layouts  184 us (8%)
  blocking collectives  57.2 us (3%)
    all_gather x1, waiting for transfers between devices, _feed_thing(): return lax.all_gather(content, axis_name=group_axis).sum(axis=0)  424 us
    psum x1, waiting for transfers between devices, per_device(): lax.psum(jnp.dot(heads_out, w_out, preferred_element_type=jnp.float32).as...  224 us
    all_gather x1, waiting for transfers between devices, per_device(): lax.all_gather(grad_after_ln.reshape(quarter_tokens, D).astype(jnp.bfloat...  116 us
    reduce_scatter x1, waiting for transfers between devices, per_device(): lax.psum_scatter(jnp.dot(grad_up_low, w_up.T, preferred_element_type=jnp....  105 us
    dot_general x1, matrix products, per_device(): jnp.dot(grad_feed, w_down.T, preferred_element_type=jnp.float32)  72.8 us
    reduce_scatter x1, waiting for transfers between devices, per_device(): lax.psum_scatter(jnp.dot(grad_proj_low, w_qkv.T, preferred_element_type=j...  66 us
    select_n x2, other arithmetic, depthwise(): jnp.where(same_item[:, :, None], moved, jnp.zeros_like(moved))  61.5 us
    convert_element_type x1, other arithmetic, per_device(): activation = act_float.astype(jnp.bfloat16)  57.2 us
  transfers between devices with their start and end apart: 13, of which 11 were waited for; matrix products, arithmetic and copies ran while one was open for 4% of the time, Pallas kernels for 0%

profile of v1, /device:TPU:0, one launch (start us, length us, event | category | flops | bytes accessed | tf_op | source)
XLA Modules:
  0.0 2186.4 jit_solution(6677423709995344879)
XLA Ops:
  53.2 38.8 %add_convert_fusion = bf16[64,64,576]{2,1,0:T(8,128)(2,1)} fusion(f32[64,64,576]{2,1,0:T(8,128)} %fusion.67, f32[576]{0:T(1024)S(1)} %get-tuple-element.161, f32[576]{0:T(1024)S(1)} %copy-done.55, f32[576]{0:T(1024)S(1)} %copy-done.57, f32[576]{0:T(1024)S(1)} %copy-done.59, f32[576]{0:T(1024)S(1)} %copy-done.61, f32[576]{0:T(1024)S(1)} %copy-done.63, ...), kind=kLoop, calls=%fused_computation.168 | loop fusion | flops 61341696 | bytes 14209280 | tf_op jit(solution)/shard_map/convert_element_type | solution.py:186
  92.1 23.2 %reshape_reshape.12 = bf16[32,2,32,2,3,3,64]{6,5,4,3,2,1,0:T(4,128)(2,1)} reshape(bf16[64,64,576]{2,1,0:T(8,128)(2,1)} %add_convert_fusion) | data formatting | bytes 9437184 | tf_op jit(solution)/shard_map/reshape;reshape | solution.py:52
  135.6 91.4 %while.24 = (s32[]{:T(128)}, bf16[4,1024,3,64]{1,3,2,0:T(8,128)(2,1)S(1)}, f32[4,1024,3]{1,2,0:T(4,128)}, bf16[4,1024,3,3,64]{1,4,2,3,0:T(8,128)(2,1)}, s32[1024]{0:T(1024)S(1)}, /*index=5*/s32[]{:T(128)}) while((s32[]{:T(128)}, bf16[4,1024,3,64]{1,3,2,0:T(8,128)(2,1)S(1)}, f32[4,1024,3]{1,2,0:T(4,128)}, ...), condition=%wide.region_5.7_spmd.clone, body=%wide.region_2.6_spmd.clone.sunk | while | flops 844297216 | bytes 45989976 | solution.py:188
  251.3 224.0 %all-reduce.43.cloned.1.call-done = bf16[4096,768]{1,0:T(8,128)(2,1)} async-done(((bf16[4096,768]{1,0:T(8,128)(2,1)}), bf16[4096,768]{1,0:T(8,128)(2,1)}) %all-reduce.43.cloned.1.call-update) | async-done | bytes 6291472 | tf_op jit(solution)/shard_map/psum | solution.py:192
  508.1 57.2 %multiply_convert_fusion.1 = (bf16[64,64,768]{2,1,0:T(8,128)(2,1)S(1)}, f32[64,64,768]{2,1,0:T(8,128)}, f32[64,64,768]{2,1,0:T(8,128)}) fusion(pred[64,64]{1,0:T(8,128)(4,1)S(1)} %copy-done.33, f32[768]{0:T(1024)S(1)} %get-tuple-element.152, pred[64,64]{1,0:T(8,128)(4,1)S(1)} %copy-done.15, f32[768]{0:T(1024)S(1)} %get-tuple-element.153, ...), kind=kLoop, calls=%fused_computation.118 | loop fusion | flops 283115520 | bytes 44100608 | tf_op jit(solution)/shard_map/convert_element_type | solution.py:206
  574.9 424.2 %all-gather.6.cloned.1.call-done = bf16[16384,768]{1,0:T(8,128)(2,1)} async-done(((bf16[4096,768]{1,0:T(8,128)(2,1)}), bf16[16384,768]{1,0:T(8,128)(2,1)}) %all-gather.6.cloned.1.call-update) | async-done | bytes 25165840 | tf_op jit(solution)/shard_map/all_gather | solution.py:14
  1031.1 72.8 %multiply_reduce_fusion.9 = (f32[768]{0:T(1024)}, f32[768]{0:T(1024)}, f32[768]{0:T(1024)}, f32[768]{0:T(1024)}, f32[768]{0:T(1024)}, /*index=5*/f32[768]{0:T(10...) fusion(f32[64,64,768]{2,1,0:T(8,128)} %fusion.65, ...), kind=kOutput, calls=%fused_computation.107 | convolution fusion | flops 4960803840 | bytes 70449152 | tf_op jit(solution)/shard_map/dot_general | solution.py:214
  1103.9 32.2 %multiply_select_fusion.8 = (f32[64,64,768]{2,1,0:T(8,128)S(1)}, f32[64,64,768]{2,1,0:T(8,128)}, f32[64,64,768]{2,1,0:T(8,128)}, f32[64,64,768]{2,1,0:T(8,128)},...) fusion(f32[64,64,768]{2,1,0:T(8,128)} %get-tuple-element.254, ...), kind=kLoop, calls=%fused_computation.116 | loop fusion | flops 47185920 | bytes 113299456 | tf_op jit(solution)/shard_map/transpose(jvp(jit(_where)))/select_n | solution.py:43
  1155.2 29.6 %fusion.47 = bf16[64,64,768]{2,1,0:T(8,128)(2,1)} fusion(f32[64,64,768]{2,1,0:T(8,128)} %get-tuple-element.210, f32[64,64,768]{2,1,0:T(8,128)} %get-tuple-element.216, f32[64,64,768]{2,1,0:T(8,128)} %get-tuple-element.217, f32[64,64,768]{2,1,0:T(8,128)} %get-tuple-element.218, f32[64,64,768]{2,1,0:T(8,128)} %get-tuple-element.219, f32[66,66,768]{2,1,0:T(8,128)} %pad_add_fusion), kind=kLoop, calls=%fused_computation.88 | loop fusion | flops 18874368 | bytes 81788928 | tf_op jit(solution)/shard_map/convert.2
  1199.6 104.5 %reduce-scatter.17.cloned.1.call-done = bf16[1024,768]{1,0:T(8,128)(2,1)} async-done(((bf16[4096,768]{1,0:T(8,128)(2,1)}), bf16[1024,768]{1,0:T(8,128)(2,1)}) %reduce-scatter.17.cloned.1.call-update) | async-done | bytes 1572880 | tf_op jit(solution)/shard_map/reduce_scatter | solution.py:219
  1312.1 115.9 %all-gather.4.cloned.1.call-done = bf16[4096,768]{1,0:T(8,128)(2,1)} async-done(((bf16[1024,768]{1,0:T(8,128)(2,1)}), bf16[4096,768]{1,0:T(8,128)(2,1)}) %all-gather.4.cloned.1.call-update) | async-done | bytes 6291472 | tf_op jit(solution)/shard_map/all_gather | solution.py:243
  1466.0 109.1 %while.25 = (s32[]{:T(128)}, f32[4,1024,3,3,64]{1,4,2,3,0:T(8,128)}, bf16[4,1024,3,3,64]{1,4,2,3,0:T(8,128)(2,1)}, f32[4,1024,3]{1,2,0:T(4,128)}, bf16[4,1024,3,...) while((s32[]{:T(128)}, f32[4,1024,3,3,64]{1,4,2,3,0:T(8,128)}, ...), condition=%wide.region_17.19_spmd.clone, body=%wide.region_15.18_spmd.clone.sunk | while | flops 2063070208 | bytes 117145728 | solution.py:270
  1588.9 26.1 %copy.60 = f32[32,2,32,2,3,3,64]{6,5,4,3,2,1,0:T(4,128)} copy(f32[32,2,32,2,3,3,64]{6,2,0,5,4,3,1:T(8,128)} %bitcast.261) | data formatting | bytes 18874368 | tf_op jit(solution)/shard_map/transpose | solution.py:62
  1615.1 26.3 %reshape_reshape.15 = f32[64,64,576]{2,1,0:T(8,128)} reshape(f32[32,2,32,2,3,3,64]{6,5,4,3,2,1,0:T(4,128)} %copy.60) | data formatting | bytes 18874368 | tf_op jit(solution)/shard_map/reshape;reshape | solution.py:274
  1641.5 42.9 %multiply_reduce_fusion.20 = (f32[576]{0:T(1024)S(1)}, f32[576]{0:T(1024)S(1)}, f32[576]{0:T(1024)S(1)}, f32[576]{0:T(1024)S(1)}, f32[576]{0:T(1024)S(1)}, /*ind...) fusion(f32[64,64,576]{2,1,0:T(8,128)} %reshape_reshape.15, ...), kind=kLoop, calls=%fused_computation.159 | loop fusion | flops 66055104 | bytes 28367360 | tf_op jit(solution)/shard_map/transpose(jvp())/reduce_sum | solution.py:43
  1684.5 29.3 %multiply_select_fusion.16 = (f32[64,64,576]{2,1,0:T(8,128)}, f32[64,64,576]{2,1,0:T(8,128)}, f32[64,64,576]{2,1,0:T(8,128)}, f32[64,64,576]{2,1,0:T(8,128)}, f3...) fusion(f32[64,64,576]{2,1,0:T(8,128)} %reshape_reshape.15, ...), kind=kLoop, calls=%fused_computation.167 | loop fusion | flops 35389440 | bytes 84981760 | tf_op jit(solution)/shard_map/transpose(jvp(jit(_where)))/select_n | solution.py:43
  1728.6 20.2 fusion.63
  1801.3 66.0 %reduce-scatter.19.cloned.1.call-done = bf16[1024,768]{1,0:T(8,128)(2,1)} async-done(((bf16[4096,768]{1,0:T(8,128)(2,1)}), bf16[1024,768]{1,0:T(8,128)(2,1)}) %reduce-scatter.19.cloned.1.call-update) | async-done | bytes 1572880 | tf_op jit(solution)/shard_map/reduce_scatter | solution.py:280
  1929.9 22.8 %reduce-scatter.33.cloned.1.call-done = f32[96,9]{1,0:T(8,128)} async-done(((f32[768,9]{1,0:T(8,128)}), f32[96,9]{1,0:T(8,128)}) %reduce-scatter.33.cloned.1.call-update) | async-done | bytes 3472
  1954.4 22.9 %all-reduce.40 = f32[9,576]{1,0:T(8,128)S(1)} all-reduce(f32[9,576]{1,0:T(8,128)S(1)} %pad_add_fusion.13), channel_id=8, replica_groups=mesh['dp'=8,'tp'=4] {'dp'}, use_global_device_ids=true, to_apply=%region_43.45.clone | all-reduce | flops 5184 | bytes 41472
  2008.5 28.7 %reduce-scatter.27.cloned.1.call-done = f32[768,96]{0,1:T(8,128)} async-done(((f32[768,768]{0,1:T(8,128)}), f32[768,96]{0,1:T(8,128)}) %reduce-scatter.27.cloned.1.call-update) | async-done | bytes 294928 | tf_op jit(solution)/shard_map/reduce_scatter | solution.py:342
  2037.2 46.1 %reduce-scatter.25.cloned.1.call-done = f32[96,768]{1,0:T(8,128)} async-done(((f32[768,768]{1,0:T(8,128)}), f32[96,768]{1,0:T(8,128)}) %reduce-scatter.25.cloned.1.call-update) | async-done | bytes 294928 | tf_op jit(solution)/shard_map/reduce_scatter | solution.py:340
  2083.3 44.2 %reduce-scatter.23.cloned.1.call-done = f32[96,576]{1,0:T(8,128)} async-done(((f32[768,576]{1,0:T(8,128)}), f32[96,576]{1,0:T(8,128)}) %reduce-scatter.23.cloned.1.call-update) | async-done | bytes 221200 | tf_op jit(solution)/shard_map/reduce_scatter | solution.py:336
  2127.5 51.9 %reduce-scatter.21.cloned.1.call-done = f32[96,1152]{1,0:T(8,128)} async-done(((f32[768,1152]{1,0:T(8,128)}), f32[96,1152]{1,0:T(8,128)}) %reduce-scatter.21.cloned.1.call-update) | async-done | bytes 442384 | tf_op jit(solution)/shard_map/reduce_scatter | solution.py:339
  (429 shorter events, 618.3 us)
Async XLA Ops:
  7.2 468.1 %all-reduce.43.cloned.1.call-start = ((), (), s32[]{:S(2)}) async-start(), calls=%async_computation.10 | async-start | bytes 12582912 | tf_op jit(solution)/shard_map/psum | solution.py:192
  245.0 230.3 %copy-start.41 = (f32[2,2,768]{2,1,0:T(2,128)S(1)}, f32[2,2,768]{2,1,0:T(2,128)}, u32[]{:S(2)}) copy-start(f32[2,2,768]{2,1,0:T(2,128)} %get-tuple-element.237) | copy-start | bytes 36868
  251.2 747.9 %all-gather.6.cloned.1.call-start = ((), (), s32[]{:S(2)}) async-start(), calls=%async_computation.18 | async-start | bytes 31457280 | tf_op jit(solution)/shard_map/all_gather | solution.py:14
  508.1 59.8 %copy-start.90 = (bf16[768,768]{1,0:T(8,128)(2,1)S(1)}, bf16[768,768]{1,0:T(8,128)(2,1)}, u32[]{:S(2)}) copy-start(bf16[768,768]{1,0:T(8,128)(2,1)} %param.33) | copy-start | bytes 3538948
  574.9 729.2 %reduce-scatter.17.cloned.1.call-start = ((), (), s32[]{:S(2)}) async-start(), calls=%async_computation.11 | async-start | bytes 7864320 | tf_op jit(solution)/shard_map/reduce_scatter | solution.py:219
  1195.0 233.0 %all-gather.4.cloned.1.call-start = ((), (), s32[]{:S(2)}) async-start(), calls=%async_computation.12 | async-start | bytes 7864320 | tf_op jit(solution)/shard_map/all_gather | solution.py:243
  1199.6 228.4 %copy-start.42 = (f32[2,2,768]{2,1,0:T(2,128)S(1)}, f32[2,2,768]{2,1,0:T(2,128)}, u32[]{:S(2)}) copy-start(f32[2,2,768]{2,1,0:T(2,128)} %get-tuple-element.237) | copy-start | bytes 36868
  1199.6 112.5 %copy-start.48 = (f32[1024]{0:T(1024)}, f32[1024]{0:T(1024)S(1)}, u32[]{:S(2)}) copy-start(f32[1024]{0:T(1024)S(1)} %broadcast_multiply_fusion.5) | copy-start | bytes 12292
  1312.0 555.3 %reduce-scatter.19.cloned.1.call-start = ((), (), s32[]{:S(2)}) async-start(), calls=%async_computation.13 | async-start | bytes 7864320 | tf_op jit(solution)/shard_map/reduce_scatter | solution.py:280
  1312.1 129.5 %copy-start.36 = (bf16[192,768]{1,0:T(8,128)(2,1)S(1)}, bf16[192,768]{1,0:T(8,128)(2,1)}, u32[]{:S(2)}) copy-start(bf16[192,768]{1,0:T(8,128)(2,1)} %param.30) | copy-start | bytes 884740
  1641.4 43.0 %copy-start.54 = (f32[576]{0:T(1024)S(1)}, f32[576]{0:T(1024)}, u32[]{:S(2)}) copy-start(f32[576]{0:T(1024)} %copy-done.53) | copy-start | bytes 6916
  1641.5 43.0 %copy-start.56 = (f32[576]{0:T(1024)S(1)}, f32[576]{0:T(1024)}, u32[]{:S(2)}) copy-start(f32[576]{0:T(1024)} %get-tuple-element.162) | copy-start | bytes 6916
  1641.5 43.0 %copy-start.58 = (f32[576]{0:T(1024)S(1)}, f32[576]{0:T(1024)}, u32[]{:S(2)}) copy-start(f32[576]{0:T(1024)} %get-tuple-element.163) | copy-start | bytes 6916
  1758.2 166.9 %reduce-scatter.29.cloned.1.call-start = ((), (), s32[]{:S(2)}) async-start(), calls=%async_computation.19 | async-start | bytes 1474560
  1791.9 75.4 %copy-start.43 = (f32[2,768]{1,0:T(2,128)S(1)}, f32[2,768]{1,0:T(2,128)}, u32[]{:S(2)}) copy-start(f32[2,768]{1,0:T(2,128)} %get-tuple-element.238) | copy-start | bytes 18436
  1886.6 66.1 %reduce-scatter.33.cloned.1.call-start = ((), (), s32[]{:S(2)}) async-start(), calls=%async_computation.21 | async-start | bytes 442368
  1887.7 114.6 %reduce-scatter.31.cloned.1.call-start = ((), (), s32[]{:S(2)}) async-start(), calls=%async_computation.20 | async-start | bytes 884736
  1894.6 142.6 %reduce-scatter.27.cloned.1.call-start = ((), (), s32[]{:S(2)}) async-start(), calls=%async_computation.17 | async-start | bytes 2654208 | tf_op jit(solution)/shard_map/reduce_scatter | solution.py:342
  1904.9 178.4 %reduce-scatter.25.cloned.1.call-start = ((), (), s32[]{:S(2)}) async-start(), calls=%async_computation.16 | async-start | bytes 2654208 | tf_op jit(solution)/shard_map/reduce_scatter | solution.py:340
  1915.2 212.3 %reduce-scatter.23.cloned.1.call-start = ((), (), s32[]{:S(2)}) async-start(), calls=%async_computation.15 | async-start | bytes 2211840 | tf_op jit(solution)/shard_map/reduce_scatter | solution.py:336
  1925.0 81.3 %copy-start.88 = (s32[32]{0:T(128)S(1)}, s32[32]{0:T(128)}, u32[]{:S(2)}) copy-start(s32[32]{0:T(128)} %param.24) | copy-start | bytes 388
  1925.0 82.4 %copy-start.89 = (s32[32]{0:T(128)S(1)}, s32[32]{0:T(128)}, u32[]{:S(2)}) copy-start(s32[32]{0:T(128)} %param.23) | copy-start | bytes 388
  1925.0 254.4 %reduce-scatter.21.cloned.1.call-start = ((), (), s32[]{:S(2)}) async-start(), calls=%async_computation.14 | async-start | bytes 3981312 | tf_op jit(solution)/shard_map/reduce_scatter | solution.py:339
  1998.2 8.0 all-to-all-start
  (88 other events, 1360.8 us)
Sparse Core Ops, SparseCore 0:
  251.3 223.9 all-reduce.42
  575.0 424.0 all-gather.5
  1195.1 108.9 reduce-scatter.16
  1312.1 115.8 all-gather.3
  1758.3 108.9 reduce-scatter.18
  1886.7 29.8 reduce-scatter.28
  1920.2 32.4 reduce-scatter.32
  1955.9 34.9 reduce-scatter.30
  1994.8 42.3 reduce-scatter.26
  2041.0 42.3 reduce-scatter.24
  2087.3 40.1 reduce-scatter.22
  2131.4 47.9 reduce-scatter.20
